TPU v7x, 32 devices: a whole 2x2x4 slice. The times are simulated.
32 devices in a mesh: row: 4 (over x, core), col: 8 (over z, y).
Axes of the slice: x: 2, y: 2, z: 4, core: 2. Of those that a mesh axis runs over, the one named last changes fastest.
Arguments:
- velocity_start: float32 [2, 256, 1024], P(None, 'row', 'col'), may hold values from -3 to 3
- stress_start: float32 [3, 256, 1024], P(None, 'row', 'col'), may hold values from -3 to 3
- wind_stress: float32 [2, 256, 1024], P(None, 'row', 'col'), may hold values from -6 to 6
- ocean_current: float32 [2, 256, 1024], P(None, 'row', 'col'), may hold values from -3 to 3
- ice_area: float32 [5, 256, 1024], P(None, 'row', 'col'), may hold values from 0.15 to 0.2
- ice_volume: float32 [5, 256, 1024], P(None, 'row', 'col'), may hold values from 0.05 to 0.6
- inverse_width: float32 [256, 1024], P('row', 'col'), may hold values from 0.7 to 1.4
- inverse_height: float32 [256, 1024], P('row', 'col'), may hold values from 0.7 to 1.4
- land_block: int32 [64, 32], P('row', 'col'), may hold values 0 or 1
- ice_block: int32 [64, 32], P('row', 'col'), may hold values 0 or 1
- writer: int32 [8], replicated, may hold values from 0 to 3
Outputs:
- velocity: float32 [2, 256, 1024], P(None, 'row', 'col')
- stress: float32 [3, 256, 1024], P(None, 'row', 'col')
- restart: float32 [4, 10, 256, 1024], P('row', None, None, 'col')
All inputs are finite; a program needn't handle non-finite values. No bound on the sum of `land_block` or of `ice_block` on one device may be relied on, other than what follows from the above.
Results may differ from a plain program's by a relative error of at most 0.00002.
Values sent between devices are 32-bit elements; how exact they have to be, the bound alone decides.
A program may use at most 64 MiB of HBM per device.

v0:
```python
import functools

import jax
import jax.numpy as jnp
from jax import lax
from jax.experimental import pallas as pl
from jax.experimental.pallas import tpu as pltpu
from jax.sharding import PartitionSpec as P

SUB = 12
PAD = 8
FIELDS = 11
STORED = 14
U, V, S, D, T, GU, GV, INERTIA, STRENGTH, HW, HH, BETA, FW, FH = range(STORED)
ALPHA = INERTIA
TINY = 1.1754944e-38

strength_scale = 4.0
hibler_decay = 20.0
mass_rate = 16.0
water_drag = 1.0
coriolis = 0.5


def halo_rows():
    return -(-SUB // 8) * 8


def slots_of(breadth):
    return breadth // SUB


def region(breadth):
    return -(-(halo_rows() // 8) * FIELDS // slots_of(breadth))


def packing(groups, breadth):
    per, tiles, deep = slots_of(breadth), region(breadth), halo_rows() // 8
    where = {}
    for k in range(deep):
        for f in range(FIELDS):
            n = k * FIELDS + f
            where[k, f] = divmod(n, per)
            where[groups - 1 - k, f] = (tiles + n // per, n % per)
    spare = [divmod(n, per) for n in range(deep * FIELDS, tiles * per)]
    free = spare + [(tiles + t, n) for t, n in spare]
    n = 0
    for k in range(deep, groups - deep):
        for f in range(FIELDS):
            m = n - len(free)
            where[k, f] = free[n] if m < 0 else (2 * tiles + m // per, m % per)
            n += 1
    return where, 1 + max(t for t, _ in where.values())


def expand_into(mask_ref, blocks_ref):
    block_cols, block_rows = blocks_ref.shape
    height, breadth = mask_ref.shape
    tall, wide = height // block_rows, breadth // block_cols
    counted = blocks_ref[...].astype(jnp.float32)
    start = wide * lax.broadcasted_iota(jnp.int32, (block_cols, breadth), 0)
    lane = lax.broadcasted_iota(jnp.int32, (block_cols, breadth), 1)
    inside = (lane >= start) & (lane < start + wide)
    for b in range(block_rows):
        spread = jnp.where(inside, counted[:, b : b + 1], 0.0)
        line = jnp.sum(spread, axis=0, keepdims=True)
        mask_ref[b * tall : (b + 1) * tall, :] = jnp.broadcast_to(line, (tall, breadth))


def kernel(
    nr,
    nc,
    vel_in,
    str_in,
    wind_in,
    cur_in,
    area_in,
    vol_in,
    iw_in,
    ih_in,
    land_in,
    ice_in,
    writer_in,
    vel_out,
    str_out,
    strips,
    writer_out,
    vel_ref,
    str_ref,
    wind_ref,
    cur_ref,
    iw_ref,
    ih_ref,
    land_ref,
    ice_ref,
    vals,
    main,
    side,
    pack_e,
    pack_w,
    land_n,
    land_s,
    mid_e,
    mid_w,
    low_e,
    low_w,
    high_e,
    high_w,
    ocean_ref,
    icy_ref,
    send_sem,
    recv_sem,
    x_send,
    x_recv,
    f_send,
    f_recv,
    in_sem,
    strip_sem,
    ring_sem,
):
    hr = halo_rows()
    height, breadth = iw_ref.shape
    cats = area_in.shape[0]
    rows = height + 2 * hr
    deep = hr // 8
    groups = height // 8
    total = rows // 8
    half = breadth // 2
    skip = total // 2 - deep
    tall = total - skip
    base = breadth - half + SUB
    cut = (base + breadth - SUB) // 2
    where, _ = packing(groups, breadth)
    tiles = region(breadth)
    r = lax.axis_index("row")
    c = lax.axis_index("col")
    east = lax.rem(c + 1, nc)
    west = lax.rem(c + nc - 1, nc)
    mirror = nc - 1 - c
    m_e = lax.rem(mirror + nc - 1, nc)
    m_w = lax.rem(mirror + 1, nc)
    partner = r + 1 - 2 * lax.rem(r, 2)
    is_top = r == nr - 1
    not_top = r < nr - 1
    above_bottom = r > 0
    self_e = jnp.logical_and(is_top, m_e == c)
    self_w = jnp.logical_and(is_top, m_w == c)
    other_e = jnp.logical_and(is_top, m_e != c)
    other_w = jnp.logical_and(is_top, m_w != c)
    others = [lax.rem(r + 2 * k, nr) for k in range(1, nr // 2)]

    own = pl.ds(pl.multiple_of(r * height, height), height)
    area_own = strips.at[0:cats, own, :]
    vol_own = strips.at[cats : 2 * cats, own, :]
    inputs = (
        (area_in, area_own),
        (vol_in, vol_own),
        (land_in, land_ref),
        (ice_in, ice_ref),
        (vel_in, vel_ref),
        (str_in, str_ref),
        (wind_in, wind_ref),
        (cur_in, cur_ref),
        (iw_in, iw_ref),
        (ih_in, ih_ref),
        (writer_in, writer_out),
    )
    arriving = [
        pltpu.make_async_copy(src, dst, in_sem.at[n]) for n, (src, dst) in enumerate(inputs)
    ]
    for copy in arriving:
        copy.start()

    barrier = pltpu.get_barrier_semaphore()

    def signal(semaphore, row, col):
        pl.semaphore_signal(
            semaphore,
            inc=1,
            device_id={"row": row, "col": col},
            device_id_type=pl.DeviceIdType.MESH,
        )

    odd = lax.rem(r, 2) == 1
    even = lax.rem(r, 2) == 0
    floor = r - lax.rem(r, 2)
    up_chip = jnp.logical_and(odd, not_top)
    down_chip = jnp.logical_and(even, above_bottom)
    along_x = jnp.logical_or(up_chip, down_chip)
    for n in range(nr // 2):
        chief = 2 * n + 1

        @pl.when(r != chief)
        def _():
            signal(barrier, chief, c)

    for beside in (east, west):
        signal(barrier, floor, beside)

        @pl.when(up_chip)
        def _():
            signal(barrier, r + 1, beside)

        @pl.when(down_chip)
        def _():
            signal(barrier, r - 2, beside)

    @pl.when(is_top)
    def _():
        signal(barrier, floor, mirror)

    @pl.when(other_e)
    def _():
        signal(barrier, floor, m_e)

    @pl.when(other_w)
    def _():
        signal(barrier, floor, m_w)

    def remote(src, dst, send, recv, row, col):
        return pltpu.make_async_remote_copy(
            src_ref=src,
            dst_ref=dst,
            send_sem=send,
            recv_sem=recv,
            device_id={"row": row, "col": col},
            device_id_type=pl.DeviceIdType.MESH,
        )

    snapshot = (area_own, vol_own)
    crossing = []
    for k, other in enumerate(others):
        for part, ref in enumerate(snapshot):
            n = 2 * k + part
            crossing.append(remote(ref, ref, x_send.at[n], x_recv.at[n], other, c))
    forwards = [
        remote(ref, ref, f_send.at[part], f_recv.at[part], partner, c)
        for part, ref in enumerate(snapshot)
    ]

    lane = lax.broadcasted_iota(jnp.int32, (8, breadth), 1)
    sub = lax.broadcasted_iota(jnp.int32, (8, breadth), 0)
    zero = jnp.zeros((8, breadth), jnp.float32)
    left_half = lane < half
    for f in range(5):
        for ref, end in ((main, PAD + rows), (side, PAD + 8 * tall)):
            ref[f, 0:PAD, :] = zero
            ref[f, end : end + PAD, :] = zero

    def roll(value, shift):
        shift = shift % breadth
        return pltpu.roll(value, shift, 1) if shift else value

    for copy in arriving:
        copy.wait()
    expand_into(ocean_ref, land_ref)
    expand_into(icy_ref, ice_ref)
    packed_e, packed_w = {}, {}
    order = list(range(deep)) + list(range(groups - 1, groups - 1 - deep, -1))
    order += list(range(deep, groups - deep))
    for k in order:
        here = slice(8 * k, 8 * k + 8)
        lines = pl.ds(pl.multiple_of(r * height + 8 * k, 8), 8)
        area = strips[0, lines, :]
        volume = strips[cats, lines, :]
        for n in range(1, cats):
            area = area + strips[n, lines, :]
            volume = volume + strips[cats + n, lines, :]
        ocean = ocean_ref[here, :]
        icy = icy_ref[here, :]
        strength = strength_scale * volume * jnp.exp(-hibler_decay * (1.0 - area)) * ocean
        inertia = mass_rate * (1.0 + volume)
        turning = coriolis * (1.0 + volume)
        damped = inertia + water_drag
        moving = ocean * icy
        live = moving / (damped * damped + turning * turning)
        ca = damped * live
        cb = turning * live
        rest = ocean * (1.0 - icy)
        cu = cur_ref[0, here, :]
        cv = cur_ref[1, here, :]
        gu = wind_ref[0, here, :] + water_drag * cu
        gv = wind_ref[1, here, :] + water_drag * cv
        s1, s2 = str_ref[0, here, :], str_ref[1, here, :]
        values = [
            vel_ref[0, here, :],
            vel_ref[1, here, :],
            s1 + s2,
            s1 - s2,
            2.0 * str_ref[2, here, :],
            ca * gu + cb * gv + rest * cu,
            ca * gv - cb * gu + rest * cv,
            moving * inertia,
            strength * (1.0 / 3.0),
            0.5 * iw_ref[here, :],
            0.5 * ih_ref[here, :],
        ]
        for f, value in enumerate(values):
            vals[f, here, :] = value
            t, n = where[k, f]
            at = n * SUB
            to_w, to_e = roll(value, at), roll(value, at + SUB)
            if t in packed_w:
                to_w = jnp.where(lane >= at, to_w, packed_w[t])
                to_e = jnp.where(lane >= at, to_e, packed_e[t])
            packed_w[t], packed_e[t] = to_w, to_e
    for t in packed_w:
        pack_w[t] = packed_w[t]
        pack_e[t] = packed_e[t]

    @pl.when(odd)
    def _():
        pl.semaphore_wait(barrier, nr - 1)
        signal(strip_sem, partner, c)

    @pl.when(even)
    def _():
        pl.semaphore_wait(strip_sem, 1)

    def halo(slot, src, dst, row, col):
        return remote(src, dst, send_sem.at[slot], recv_sem.at[slot], row, col)

    bottom = slice(0, tiles)
    upper = slice(tiles, 2 * tiles)
    vals_top = vals.at[:, height - hr : height, :]
    vals_bottom = vals.at[:, 0:hr, :]
    to_west = halo(0, pack_w, mid_e, r, west)
    to_east = halo(1, pack_e, mid_w, r, east)
    up = [
        halo(2, vals_top, land_s, r + 1, c),
        halo(4, pack_w.at[upper], low_e, r + 1, west),
        halo(5, pack_e.at[upper], low_w, r + 1, east),
    ]
    down = [
        halo(3, vals_bottom, land_n, r - 1, c),
        halo(6, pack_w.at[bottom], high_e, r - 1, west),
        halo(7, pack_e.at[bottom], high_w, r - 1, east),
    ]
    over = remote(vals_top, land_n, send_sem.at[8], recv_sem.at[3], r, mirror)
    over_w = remote(pack_w.at[upper], high_e, send_sem.at[9], recv_sem.at[6], r, m_w)
    over_e = remote(pack_e.at[upper], high_w, send_sem.at[10], recv_sem.at[7], r, m_e)

    @pl.when(not_top)
    def _():
        up[0].start()

    @pl.when(above_bottom)
    def _():
        down[0].start()

    @pl.when(jnp.logical_not(along_x))
    def _():
        for copy in crossing:
            copy.start()

    for copy in forwards:
        copy.start()

    @pl.when(even)
    def _():
        top_chip = (r == nr - 2).astype(jnp.int32)
        peers = 4 + 2 * above_bottom.astype(jnp.int32) + 2 - 2 * top_chip + top_chip
        peers = peers + top_chip * (m_e != c).astype(jnp.int32)
        peers = peers + top_chip * (m_w != c).astype(jnp.int32)
        pl.semaphore_wait(barrier, peers)
        signal(ring_sem, partner, c)

    @pl.when(odd)
    def _():
        pl.semaphore_wait(ring_sem, 1)

    @pl.when(self_w)
    def _():
        high_e[...] = pack_w[upper]

    @pl.when(self_e)
    def _():
        high_w[...] = pack_e[upper]

    def send_beside(mid, across, other, folded):
        mid.start()

        @pl.when(not_top)
        def _():
            up[across].start()

        @pl.when(above_bottom)
        def _():
            down[across].start()

        @pl.when(other)
        def _():
            folded.start()

    odd_col = lax.rem(c, 2) == 1

    @pl.when(odd_col)
    def _():
        send_beside(to_east, 2, other_e, over_e)

    send_beside(to_west, 1, other_w, over_w)

    @pl.when(jnp.logical_not(odd_col))
    def _():
        send_beside(to_east, 2, other_e, over_e)

    @pl.when(is_top)
    def _():
        over.start()

    @pl.when(along_x)
    def _():
        for copy in crossing:
            copy.start()

    def tile(g):
        return slice(PAD + 8 * g, PAD + 8 * g + 8)

    def homes(g):
        return [(b, n) for b, n in ((g, 0), (g - skip, 1)) if 0 <= b < tall]

    def fill(g, f, value):
        main[f, tile(g), :] = roll(value, SUB)
        for b, right in homes(g):
            mask = lane >= half if right else left_half
            pltpu.store(side.at[f, tile(b), :], roll(value, right * half - base), mask=mask)

    for k in range(groups):
        for f in range(FIELDS):
            fill(deep + k, f, vals[f, 8 * k : 8 * k + 8, :])

    @pl.when(r == 0)
    def _():
        land_s[...] = jnp.zeros(land_s.shape, jnp.float32)
        low_e[...] = jnp.zeros(low_e.shape, jnp.float32)
        low_w[...] = jnp.zeros(low_w.shape, jnp.float32)

    swap = is_top.astype(jnp.int32)

    @pl.when(above_bottom)
    def _():
        up[0].wait_recv()

    @pl.when(not_top)
    def _():
        down[0].wait_recv()

    @pl.when(is_top)
    def _():
        over.wait_recv()

    for g in range(deep):
        line = g + swap * (deep - 1 - 2 * g)
        from_n = pl.ds(pl.multiple_of(8 * line, 8), 8)
        for f in range(FIELDS):
            fill(g, f, land_s[f, 8 * g : 8 * g + 8, :])
            fill(deep + groups + g, f, land_n[f, from_n, :])

    def edges(low, mid, high):
        for g in range(total):
            if g < deep:
                k, source, first = groups - deep + g, low, tiles
            elif g < deep + groups:
                k, source, first = g - deep, mid, 0
            else:
                k, source, first = g - deep - groups, high, 0
            for f in range(FIELDS):
                t, n = where[k, f]
                yield g, f, source[t - first], n * SUB

    to_west.wait_recv()

    @pl.when(above_bottom)
    def _():
        up[1].wait_recv()

    @pl.when(not_top)
    def _():
        down[1].wait_recv()

    @pl.when(other_w)
    def _():
        over_w.wait_recv()

    for g, f, value, at in edges(low_e, mid_e, high_e):
        for b, right in homes(g):
            to = right * half + half - SUB
            mask = (lane >= to) & (lane < to + SUB)
            pltpu.store(side.at[f, tile(b), :], roll(value, to - at), mask=mask)

    to_east.wait_recv()

    @pl.when(above_bottom)
    def _():
        up[2].wait_recv()

    @pl.when(not_top)
    def _():
        down[2].wait_recv()

    @pl.when(other_e)
    def _():
        over_e.wait_recv()

    for g, f, value, at in edges(low_w, mid_w, high_w):
        pltpu.store(main.at[f, tile(g), :], roll(value, -at), mask=lane < SUB)

    turn = coriolis / mass_rate
    for ref, count in ((main, total), (side, tall)):
        for g in range(count):
            here = slice(PAD + 8 * g, PAD + 8 * g + 8)
            inertia = ref[INERTIA, here, :]
            damped = inertia + water_drag
            turning = turn * inertia
            scaled = inertia / (damped * damped + turning * turning)
            inverse = 0.5 / jnp.maximum(inertia, 1.0)
            ref[ALPHA, here, :] = damped * scaled
            ref[BETA, here, :] = turning * scaled
            ref[FW, here, :] = inverse * ref[HW, here, :]
            ref[FH, here, :] = inverse * ref[HH, here, :]

    near = deep + groups
    near_first = PAD + 8 * near
    own_top = near_first - 1
    shift = 8 * skip
    fold_south = (sub == 0) & is_top
    fold_north = (sub == 7) & is_top
    fold_south_side = fold_south & (lane >= half)
    fold_north_side = fold_north & (lane >= half)
    last_line = sub == 7

    def spread(ref, f, at):
        return jnp.broadcast_to(ref[f, at : at + 1, :], (8, breadth))

    def stress_tile(ref, g, folded, far):
        here = slice(PAD + 8 * g, PAD + 8 * g + 8)
        south = slice(PAD + 8 * g - 1, PAD + 8 * g + 7)
        u, v = ref[U, here, :], ref[V, here, :]
        su, sv = ref[U, south, :], ref[V, south, :]
        if folded is not None:
            su = jnp.where(folded, spread(ref, U, far), su)
            sv = jnp.where(folded, spread(ref, V, far), sv)
        us, ud, vs, vd = u + su, u - su, v + sv, v - sv
        du, dv = us - pltpu.roll(us, 1, 1), vs - pltpu.roll(vs, 1, 1)
        eu, ev = ud + pltpu.roll(ud, 1, 1), vd + pltpu.roll(vd, 1, 1)
        hw, hh = ref[HW, here, :], ref[HH, here, :]
        gux, gvy = hw * du, hh * ev
        div, ten, shear = gux + gvy, gux - gvy, hw * dv + hh * eu
        ten4, shear4 = 0.25 * ten, 0.25 * shear
        square = div * div + (ten4 * ten + shear4 * shear)
        deform = square * lax.rsqrt(jnp.maximum(square, TINY))
        w = ref[STRENGTH, here, :] / (deform + 0.5)
        c = div - deform
        ref[S, here, :] = ref[S, here, :] * (2.0 / 3.0) + w * (c + ten4)
        ref[D, here, :] = ref[D, here, :] * (2.0 / 3.0) + w * (c - ten4)
        ref[T, here, :] = ref[T, here, :] * (2.0 / 3.0) + w * shear4

    def velocity_tile(ref, g, folded=None, ghost=None, last=None):
        here = slice(PAD + 8 * g, PAD + 8 * g + 8)
        north = slice(PAD + 8 * g + 1, PAD + 8 * g + 9)
        s, d, t = ref[S, here, :], ref[D, here, :], ref[T, here, :]
        ns, nd, nt = ref[S, north, :], ref[D, north, :], ref[T, north, :]
        if last is not None:
            ns, nd, nt = (
                jnp.where(last_line, spread(ref, f, last), n)
                for f, n in ((S, ns), (D, nd), (T, nt))
            )
        if folded is not None:
            ns, nd, nt = (jnp.where(folded, 0.0, n) for n in (ns, nd, nt))
        ps, dt, pt, dd = s + ns, nt - t, t + nt, nd - d
        back = breadth - 1
        es, et = pltpu.roll(ps, back, 1) - ps, dt + pltpu.roll(dt, back, 1)
        ft, fd = pltpu.roll(pt, back, 1) - pt, dd + pltpu.roll(dd, back, 1)
        if folded is not None:
            es, et, ft, fd = (
                value + jnp.where(folded, line, 0.0)
                for value, line in zip((es, et, ft, fd), ghost)
            )
        fw, fh = ref[FW, here, :], ref[FH, here, :]
        x = ref[U, here, :] + (fw * es + fh * et)
        y = ref[V, here, :] + (fw * ft + fh * fd)
        alpha, beta = ref[ALPHA, here, :], ref[BETA, here, :]
        ref[U, here, :] = alpha * x + beta * y + ref[GU, here, :]
        ref[V, here, :] = alpha * y - beta * x + ref[GV, here, :]

    def mirrored(reach, line):
        index = reach - lane
        return jnp.take_along_axis(line, jnp.where(index < 0, index + breadth, index), axis=1)

    from_side = lane <= breadth - 1 + SUB - cut
    from_side_e = lane < breadth - 1 + SUB - cut

    def fold():
        def stack(ref, back):
            lines = [
                ref[f, at - back : at - back + 1, :]
                for at in (own_top, own_top + 8)
                for f in (S, D, T)
            ]
            return jnp.concatenate(lines + lines[:2], axis=0)

        a, b = stack(main, 0), stack(side, shift)
        last = breadth - 1
        turned, turned_e = mirrored(last, a), mirrored(last - 1, a)
        moved, moved_e = mirrored(last + 2 * SUB, a), mirrored(last - 1 + 2 * SUB, a)
        sides, sides_e = mirrored(last, b), mirrored(last - 1, b)
        moved = jnp.where(from_side, sides, moved)
        moved_e = jnp.where(from_side_e, sides_e, moved_e)
        found = []
        for here, far in ((moved, moved_e), (turned, turned_e)):
            less, more = far - here, far + here
            for first in (3, 0):
                picked = ((less, 0), (more, 2), (less, 2), (more, 1))
                found.append(
                    [
                        jnp.broadcast_to(x[first + f : first + f + 1, :], (8, breadth))
                        for x, f in picked
                    ]
                )
        return found

    def cycle(first, stresses, velocities):
        def body(_, carry):
            for g in range(first, total):
                if g < stresses:
                    on = g == near
                    far = near_first + 15
                    stress_tile(main, g, fold_south if on else None, far)
                    if g < tall - first:
                        on = g == near - skip
                        stress_tile(side, g, fold_south_side if on else None, far - shift)
            ghosts = fold()
            for g in range(first, velocities):
                if g in (near - 1, near):
                    velocity_tile(main, g, fold_north, ghosts[g - near + 1])
                else:
                    velocity_tile(main, g, last=near_first if g == total - 1 else None)
                b = g + skip
                if g < tall - first:
                    if b in (near - 1, near):
                        velocity_tile(side, g, fold_north_side, ghosts[2 + b - near + 1])
                    else:
                        last = near_first - shift if g == tall - 1 else None
                        velocity_tile(side, g, last=last)
            return carry

        return body

    def relay(k, part):
        source = lax.rem(r + nr - 2 * (k + 1), nr)
        lines = pl.ds(pl.multiple_of(source * height, height), height)
        block = strips.at[part * cats : (part + 1) * cats, lines, :]
        slot = 2 + 2 * k + part
        return remote(block, block, f_send.at[slot], f_recv.at[slot], partner, c)

    relays = [relay(k, part) for k in range(len(others)) for part in range(2)]

    def pass_on(parts, early):
        for k in range(len(others)):
            source = lax.rem(r + nr - 2 * (k + 1), nr)
            outer = jnp.logical_or(source == 0, source == nr - 1)

            @pl.when(outer if early else jnp.logical_not(outer))
            def _():
                for part in parts:
                    crossing[2 * k + part].wait_recv()
                    relays[2 * k + part].start()

    wide = SUB - 8
    lax.fori_loop(0, wide, cycle(0, total, total), 0)
    pass_on((0, 1), True)
    lax.fori_loop(0, 4, cycle(1, total - 1, total - 1), 0)
    pass_on((0,), False)
    lax.fori_loop(0, SUB - wide - 5, cycle(1, total - 1, total - 1), 0)
    pass_on((1,), False)
    cycle(1, total - 1, near)(0, 0)

    keep = lane < cut
    for k in range(groups):
        b, right = homes(deep + k)[-1 if 2 * k >= groups else 0]
        out = []
        for f in (U, V, S, D, T):
            a = roll(main[f, tile(deep + k), :], -SUB)
            z = roll(side[f, tile(b), :], base - right * half)
            out.append(jnp.where(keep, a, z))
        at = slice(8 * k, 8 * k + 8)
        vel_out[0, at, :] = out[0]
        vel_out[1, at, :] = out[1]
        str_out[0, at, :] = 0.5 * (out[2] + out[3])
        str_out[1, at, :] = 0.5 * (out[2] - out[3])
        str_out[2, at, :] = 0.5 * out[4]

    to_west.wait_send()
    to_east.wait_send()

    @pl.when(not_top)
    def _():
        for copy in up:
            copy.wait_send()

    @pl.when(above_bottom)
    def _():
        for copy in down:
            copy.wait_send()

    @pl.when(is_top)
    def _():
        over.wait_send()

    @pl.when(other_w)
    def _():
        over_w.wait_send()

    @pl.when(other_e)
    def _():
        over_e.wait_send()

    for copy in crossing:
        copy.wait_send()
    for copy in forwards + relays:
        copy.wait()


def place(strips, vel, stress, writer, restart_out, vel_out, str_out, blank, sem):
    r = lax.axis_index("row")
    c = lax.axis_index("col")
    small = [
        pltpu.make_async_copy(vel, vel_out, sem.at[0]),
        pltpu.make_async_copy(stress, str_out, sem.at[1]),
    ]
    for copy in small:
        copy.start()
    index = lax.broadcasted_iota(jnp.int32, writer.shape, 1)
    chosen = jnp.sum(jnp.where(index == c, writer[...], 0))
    fields = strips.shape[0]

    @pl.when(chosen == r)
    def _():
        copies = [
            pltpu.make_async_copy(strips.at[n], restart_out.at[0, n], sem.at[2 + n])
            for n in range(fields)
        ]
        for copy in copies:
            copy.start()
        for copy in copies:
            copy.wait()

    @pl.when(chosen != r)
    def _():
        blank[...] = jnp.zeros(blank.shape, blank.dtype)
        copies = [
            pltpu.make_async_copy(blank, restart_out.at[0, n], sem.at[2 + n])
            for n in range(fields)
        ]
        for copy in copies:
            copy.start()
        for copy in copies:
            copy.wait()

    for copy in small:
        copy.wait()


def shards(nr, nc, *operands):
    (vel, stress, wind, current, area, volume, iw, ih, land, ice, writer) = operands
    hr = halo_rows()
    height, breadth = iw.shape
    cats = area.shape[0]
    rows = height + 2 * hr
    _, packed = packing(height // 8, breadth)
    vmem = pl.BlockSpec(memory_space=pltpu.VMEM)
    hbm = pl.BlockSpec(memory_space=pltpu.HBM)
    relayed = max(2 * (nr // 2 - 1), 1)
    f32 = jnp.float32
    land, ice = land.T, ice.T
    writer = writer[None]
    inputs = [
        pltpu.with_memory_space_constraint(x, pltpu.HBM)
        for x in (vel, stress, wind, current, area, volume, iw, ih, land, ice, writer)
    ]
    sent = 4 * (2 * FIELDS * hr * breadth + 20 * packed * breadth + 3 * area.size)
    velocity, stresses, strips, writer = pl.pallas_call(
        functools.partial(kernel, nr, nc),
        out_shape=(
            jax.ShapeDtypeStruct(vel.shape, f32),
            jax.ShapeDtypeStruct(stress.shape, f32),
            jax.ShapeDtypeStruct((2 * cats, nr * height, breadth), f32),
            jax.ShapeDtypeStruct(writer.shape, writer.dtype),
        ),
        in_specs=[hbm] * 11,
        out_specs=(vmem,) * 4,
        scratch_shapes=[
            pltpu.VMEM(vel.shape, f32),
            pltpu.VMEM(stress.shape, f32),
            pltpu.VMEM(wind.shape, f32),
            pltpu.VMEM(current.shape, f32),
            pltpu.VMEM(iw.shape, f32),
            pltpu.VMEM(ih.shape, f32),
            pltpu.VMEM(land.shape, land.dtype),
            pltpu.VMEM(ice.shape, ice.dtype),
            pltpu.VMEM((FIELDS, height, breadth), f32),
            pltpu.VMEM((STORED, rows + 2 * PAD, breadth), f32),
            pltpu.VMEM((STORED, rows // 2 + hr + 2 * PAD, breadth), f32),
            *[pltpu.VMEM((packed, 8, breadth), f32)] * 2,
            *[pltpu.VMEM((FIELDS, hr, breadth), f32)] * 2,
            *[pltpu.VMEM((packed, 8, breadth), f32)] * 2,
            *[pltpu.VMEM((region(breadth), 8, breadth), f32)] * 4,
            pltpu.VMEM((height, breadth), f32),
            pltpu.VMEM((height, breadth), f32),
            pltpu.SemaphoreType.DMA((11,)),
            pltpu.SemaphoreType.DMA((8,)),
            pltpu.SemaphoreType.DMA((relayed,)),
            pltpu.SemaphoreType.DMA((relayed,)),
            pltpu.SemaphoreType.DMA((2 + relayed,)),
            pltpu.SemaphoreType.DMA((2 + relayed,)),
            pltpu.SemaphoreType.DMA((11,)),
            pltpu.SemaphoreType.REGULAR,
            pltpu.SemaphoreType.REGULAR,
        ],
        compiler_params=pltpu.CompilerParams(
            collective_id=0, has_side_effects=True, vmem_limit_bytes=32 * 1024 * 1024
        ),
        cost_estimate=pl.CostEstimate(
            flops=SUB * rows * breadth * 200, bytes_accessed=sent, transcendentals=0
        ),
    )(*inputs)
    restart, velocity, stresses = pl.pallas_call(
        place,
        out_shape=(
            jax.ShapeDtypeStruct((1,) + strips.shape, f32),
            jax.ShapeDtypeStruct(vel.shape, f32),
            jax.ShapeDtypeStruct(stress.shape, f32),
        ),
        in_specs=[vmem] * 4,
        out_specs=(hbm,) * 3,
        scratch_shapes=[
            pltpu.VMEM(strips.shape[1:], f32),
            pltpu.SemaphoreType.DMA((2 + 2 * cats,)),
        ],
        compiler_params=pltpu.CompilerParams(vmem_limit_bytes=4 * 1024 * 1024),
    )(strips, velocity, stresses, writer)
    return velocity, stresses, restart


def solution(mesh):
    field = P(None, "row", "col")
    flat = P("row", "col")
    return jax.shard_map(
        functools.partial(shards, mesh.shape["row"], mesh.shape["col"]),
        mesh=mesh,
        in_specs=(field,) * 6 + (flat,) * 4 + (P(),),
        out_specs=(field, field, P("row", None, None, "col")),
        check_vma=False,
    )
```

profile of v0, /device:TPU:0, one launch (start us, length us, event | category | flops | bytes accessed | tf_op | source)
XLA Modules:
  0.0 17.3 jit_solution(6530934280089840613)
XLA Ops:
  0.6 15.4 %shard_map.130 = (f32[2,64,128]{2,1,0:T(8,128)S(1)}, f32[3,64,128]{2,1,0:T(8,128)S(1)}, f32[10,256,128]{2,1,0:T(8,128)S(1)}, s32[1,8]{1,0:T(1,128)S(1)}) custom-call(f32[2,64,128]{2,1,0:T(8,128)} %vel_in.1, f32[3,64,128]{2,1,0:T(8,128)} %str_in.1, f32[2,64,128]{2,1,0:T(8,128)} %wind_in.1, f32[2,64,128]{2,1,0:T(8,128)} %cur_in.1, f32[5,64,128]{2,1,0:T(8,128)} %area_in.1, ...), custom_call_target="tpu_custom_call" | custom-call | flops 29491200 | bytes 763904 | tf_op jit(solution)/shard_map/pallas_call | solution.py:782
  16.0 1.3 %shard_map.131 = (f32[1,10,256,128]{3,2,1,0:T(8,128)}, f32[2,64,128]{2,1,0:T(8,128)}, f32[3,64,128]{2,1,0:T(8,128)}) custom-call(f32[10,256,128]{2,1,0:T(8,128)S(1)} %get-tuple-element.10.strips, f32[2,64,128]{2,1,0:T(8,128)S(1)} %get-tuple-element.11.vel, f32[3,64,128]{2,1,0:T(8,128)S(1)} %get-tuple-element.12.stress, s32[1,8]{1,0:T(1,128)S(1)} %get-tuple-element.13.writer), custom_call_target="tpu_custom_call" | custom-call | tf_op jit(solution)/shard_map/pallas_call | solution.py:827
where the time goes:
time: 17.6 us; the launch traced here: 17.3 us
  Pallas kernels  16.7 us (95%)
  between operations  0.64 us (4%)
    pallas_call x1, Pallas kernels, shards(): pl.pallas_call(functools.partial(kernel, nr, nc), out_shape=(jax.ShapeDty...  15.4 us
    pallas_call x1, Pallas kernels, shards(): pl.pallas_call(place, out_shape=(jax.ShapeDtypeStruct((1,) + strips.shape...  1.31 us

commit v1 on v0

--- a/solution.py
+++ b/solution.py
@@ -10,9 +10,10 @@
 SUB = 12
 PAD = 8
 FIELDS = 11
-STORED = 14
-U, V, S, D, T, GU, GV, INERTIA, STRENGTH, HW, HH, BETA, FW, FH = range(STORED)
+STORED = 22
+U, V, S, D, T, GU, GV, INERTIA, STRENGTH, HW, HH, BETA, FW, FH, *DIFFS = range(STORED)
 ALPHA = INERTIA
+AU, BU, AV, BV, AS, BT, AT, BD = DIFFS
 TINY = 1.1754944e-38
 
 strength_scale = 4.0
@@ -251,11 +252,52 @@
         shift = shift % breadth
         return pltpu.roll(value, shift, 1) if shift else value
 
-    for copy in arriving:
+    @pl.when(odd)
+    def _():
+        pl.semaphore_wait(barrier, nr - 1)
+        signal(strip_sem, partner, c)
+
+    for copy in arriving[:2]:
         copy.wait()
+
+    @pl.when(jnp.logical_and(odd, jnp.logical_not(along_x)))
+    def _():
+        for copy in crossing:
+            copy.start()
+
+    @pl.when(odd)
+    def _():
+        for copy in forwards:
+            copy.start()
+
+    for copy in arriving[2:]:
+        copy.wait()
+    def halo(slot, src, dst, row, col):
+        return remote(src, dst, send_sem.at[slot], recv_sem.at[slot], row, col)
+
+    bottom = slice(0, tiles)
+    upper = slice(tiles, 2 * tiles)
+    vals_top = vals.at[:, height - hr : height, :]
+    vals_bottom = vals.at[:, 0:hr, :]
+    to_west = halo(0, pack_w, mid_e, r, west)
+    to_east = halo(1, pack_e, mid_w, r, east)
+    up = [
+        halo(2, vals_top, land_s, r + 1, c),
+        halo(4, pack_w.at[upper], low_e, r + 1, west),
+        halo(5, pack_e.at[upper], low_w, r + 1, east),
+    ]
+    down = [
+        halo(3, vals_bottom, land_n, r - 1, c),
+        halo(6, pack_w.at[bottom], high_e, r - 1, west),
+        halo(7, pack_e.at[bottom], high_w, r - 1, east),
+    ]
+    over = remote(vals_top, land_n, send_sem.at[8], recv_sem.at[3], r, mirror)
+    over_w = remote(pack_w.at[upper], high_e, send_sem.at[9], recv_sem.at[6], r, m_w)
+    over_e = remote(pack_e.at[upper], high_w, send_sem.at[10], recv_sem.at[7], r, m_e)
+
     expand_into(ocean_ref, land_ref)
     expand_into(icy_ref, ice_ref)
-    packed_e, packed_w = {}, {}
+    packed_e, packed_w, first_e = {}, {}, {}
     order = list(range(deep)) + list(range(groups - 1, groups - 1 - deep, -1))
     order += list(range(deep, groups - deep))
     for k in order:
@@ -299,47 +341,20 @@
             vals[f, here, :] = value
             t, n = where[k, f]
             at = n * SUB
-            to_w, to_e = roll(value, at), roll(value, at + SUB)
-            if t in packed_w:
-                to_w = jnp.where(lane >= at, to_w, packed_w[t])
-                to_e = jnp.where(lane >= at, to_e, packed_e[t])
-            packed_w[t], packed_e[t] = to_w, to_e
+            turned = roll(value, at)
+            packed_w[t] = jnp.where(lane >= at, turned, packed_w[t]) if t in packed_w else turned
+            if n:
+                packed_e[t] = jnp.where(lane >= at - SUB, turned, packed_e[t])
+            else:
+                packed_e[t] = first_e[t] = turned
     for t in packed_w:
         pack_w[t] = packed_w[t]
-        pack_e[t] = packed_e[t]
-
-    @pl.when(odd)
-    def _():
-        pl.semaphore_wait(barrier, nr - 1)
-        signal(strip_sem, partner, c)
+        pack_e[t] = jnp.where(lane >= breadth - SUB, first_e[t], packed_e[t])
 
     @pl.when(even)
     def _():
         pl.semaphore_wait(strip_sem, 1)
 
-    def halo(slot, src, dst, row, col):
-        return remote(src, dst, send_sem.at[slot], recv_sem.at[slot], row, col)
-
-    bottom = slice(0, tiles)
-    upper = slice(tiles, 2 * tiles)
-    vals_top = vals.at[:, height - hr : height, :]
-    vals_bottom = vals.at[:, 0:hr, :]
-    to_west = halo(0, pack_w, mid_e, r, west)
-    to_east = halo(1, pack_e, mid_w, r, east)
-    up = [
-        halo(2, vals_top, land_s, r + 1, c),
-        halo(4, pack_w.at[upper], low_e, r + 1, west),
-        halo(5, pack_e.at[upper], low_w, r + 1, east),
-    ]
-    down = [
-        halo(3, vals_bottom, land_n, r - 1, c),
-        halo(6, pack_w.at[bottom], high_e, r - 1, west),
-        halo(7, pack_e.at[bottom], high_w, r - 1, east),
-    ]
-    over = remote(vals_top, land_n, send_sem.at[8], recv_sem.at[3], r, mirror)
-    over_w = remote(pack_w.at[upper], high_e, send_sem.at[9], recv_sem.at[6], r, m_w)
-    over_e = remote(pack_e.at[upper], high_w, send_sem.at[10], recv_sem.at[7], r, m_e)
-
     @pl.when(not_top)
     def _():
         up[0].start()
@@ -348,13 +363,15 @@
     def _():
         down[0].start()
 
-    @pl.when(jnp.logical_not(along_x))
+    @pl.when(jnp.logical_and(even, jnp.logical_not(along_x)))
     def _():
         for copy in crossing:
             copy.start()
 
-    for copy in forwards:
-        copy.start()
+    @pl.when(even)
+    def _():
+        for copy in forwards:
+            copy.start()
 
     @pl.when(even)
     def _():
@@ -456,68 +473,65 @@
             fill(g, f, land_s[f, 8 * g : 8 * g + 8, :])
             fill(deep + groups + g, f, land_n[f, from_n, :])
 
-    def edges(low, mid, high):
-        for g in range(total):
-            if g < deep:
-                k, source, first = groups - deep + g, low, tiles
-            elif g < deep + groups:
-                k, source, first = g - deep, mid, 0
-            else:
-                k, source, first = g - deep - groups, high, 0
+    def edges(span, source, first, origin):
+        for g in span:
             for f in range(FIELDS):
-                t, n = where[k, f]
+                t, n = where[g - origin, f]
                 yield g, f, source[t - first], n * SUB
 
+    lows, mids = range(deep), range(deep, deep + groups)
+    highs = range(deep + groups, total)
+    spans = ((mids, 0, deep), (lows, tiles, deep - groups), (highs, 0, deep + groups))
+    turn = coriolis / mass_rate
+
+    def derive(ref, here):
+        inertia = ref[INERTIA, here, :]
+        damped = inertia + water_drag
+        turning = turn * inertia
+        scaled = inertia / (damped * damped + turning * turning)
+        inverse = 0.5 / jnp.maximum(inertia, 1.0)
+        ref[ALPHA, here, :] = damped * scaled
+        ref[BETA, here, :] = turning * scaled
+        ref[FW, here, :] = inverse * ref[HW, here, :]
+        ref[FH, here, :] = inverse * ref[HH, here, :]
+
+    def await_low(n):
+        @pl.when(above_bottom)
+        def _():
+            up[n].wait_recv()
+
+    def await_high(n, other, folded):
+        @pl.when(not_top)
+        def _():
+            down[n].wait_recv()
+
+        @pl.when(other)
+        def _():
+            folded.wait_recv()
+
     to_west.wait_recv()
-
-    @pl.when(above_bottom)
-    def _():
-        up[1].wait_recv()
-
-    @pl.when(not_top)
-    def _():
-        down[1].wait_recv()
-
-    @pl.when(other_w)
-    def _():
-        over_w.wait_recv()
-
-    for g, f, value, at in edges(low_e, mid_e, high_e):
-        for b, right in homes(g):
-            to = right * half + half - SUB
-            mask = (lane >= to) & (lane < to + SUB)
-            pltpu.store(side.at[f, tile(b), :], roll(value, to - at), mask=mask)
-
-    to_east.wait_recv()
-
-    @pl.when(above_bottom)
-    def _():
-        up[2].wait_recv()
-
-    @pl.when(not_top)
-    def _():
-        down[2].wait_recv()
-
-    @pl.when(other_e)
-    def _():
-        over_e.wait_recv()
-
-    for g, f, value, at in edges(low_w, mid_w, high_w):
-        pltpu.store(main.at[f, tile(g), :], roll(value, -at), mask=lane < SUB)
-
-    turn = coriolis / mass_rate
-    for ref, count in ((main, total), (side, tall)):
-        for g in range(count):
-            here = slice(PAD + 8 * g, PAD + 8 * g + 8)
-            inertia = ref[INERTIA, here, :]
-            damped = inertia + water_drag
-            turning = turn * inertia
-            scaled = inertia / (damped * damped + turning * turning)
-            inverse = 0.5 / jnp.maximum(inertia, 1.0)
-            ref[ALPHA, here, :] = damped * scaled
-            ref[BETA, here, :] = turning * scaled
-            ref[FW, here, :] = inverse * ref[HW, here, :]
-            ref[FH, here, :] = inverse * ref[HH, here, :]
+    await_low(1)
+    await_high(1, other_w, over_w)
+    for source, span in zip((mid_e, low_e, high_e), spans):
+        for g, f, value, at in edges(span[0], source, *span[1:]):
+            for b, right in homes(g):
+                to = right * half + half - SUB
+                mask = (lane >= to) & (lane < to + SUB)
+                pltpu.store(side.at[f, tile(b), :], roll(value, to - at), mask=mask)
+    for b in range(tall):
+        derive(side, tile(b))
+
+    for n, (source, span) in enumerate(zip((mid_w, low_w, high_w), spans)):
+        if n == 0:
+            to_east.wait_recv()
+        elif n == 1:
+            await_low(2)
+        else:
+            await_high(2, other_e, over_e)
+        for g, f, value, at in edges(span[0], source, *span[1:]):
+            pltpu.store(main.at[f, tile(g), :], roll(value, SUB - at), mask=lane < SUB)
+        for g in span[0]:
+            derive(main, tile(g))
 
     near = deep + groups
     near_first = PAD + 8 * near
@@ -532,17 +546,26 @@
     def spread(ref, f, at):
         return jnp.broadcast_to(ref[f, at : at + 1, :], (8, breadth))
 
+    def differ_velocity(ref, g):
+        here = tile(g)
+        u, v = ref[U, here, :], ref[V, here, :]
+        wu, wv = pltpu.roll(u, 1, 1), pltpu.roll(v, 1, 1)
+        ref[AU, here, :] = u - wu
+        ref[BU, here, :] = u + wu
+        ref[AV, here, :] = v - wv
+        ref[BV, here, :] = v + wv
+
     def stress_tile(ref, g, folded, far):
-        here = slice(PAD + 8 * g, PAD + 8 * g + 8)
+        here = tile(g)
         south = slice(PAD + 8 * g - 1, PAD + 8 * g + 7)
-        u, v = ref[U, here, :], ref[V, here, :]
-        su, sv = ref[U, south, :], ref[V, south, :]
+        below = [ref[f, south, :] for f in (AU, BU, AV, BV)]
         if folded is not None:
-            su = jnp.where(folded, spread(ref, U, far), su)
-            sv = jnp.where(folded, spread(ref, V, far), sv)
-        us, ud, vs, vd = u + su, u - su, v + sv, v - sv
-        du, dv = us - pltpu.roll(us, 1, 1), vs - pltpu.roll(vs, 1, 1)
-        eu, ev = ud + pltpu.roll(ud, 1, 1), vd + pltpu.roll(vd, 1, 1)
+            below = [
+                jnp.where(folded, spread(ref, f, far), x)
+                for f, x in zip((AU, BU, AV, BV), below)
+            ]
+        du, eu = ref[AU, here, :] + below[0], ref[BU, here, :] - below[1]
+        dv, ev = ref[AV, here, :] + below[2], ref[BV, here, :] - below[3]
         hw, hh = ref[HW, here, :], ref[HH, here, :]
         gux, gvy = hw * du, hh * ev
         div, ten, shear = gux + gvy, gux - gvy, hw * dv + hh * eu
@@ -551,31 +574,30 @@
         deform = square * lax.rsqrt(jnp.maximum(square, TINY))
         w = ref[STRENGTH, here, :] / (deform + 0.5)
         c = div - deform
-        ref[S, here, :] = ref[S, here, :] * (2.0 / 3.0) + w * (c + ten4)
-        ref[D, here, :] = ref[D, here, :] * (2.0 / 3.0) + w * (c - ten4)
-        ref[T, here, :] = ref[T, here, :] * (2.0 / 3.0) + w * shear4
+        s = ref[S, here, :] * (2.0 / 3.0) + w * (c + ten4)
+        d = ref[D, here, :] * (2.0 / 3.0) + w * (c - ten4)
+        t = ref[T, here, :] * (2.0 / 3.0) + w * shear4
+        ref[S, here, :] = s
+        ref[D, here, :] = d
+        ref[T, here, :] = t
+        back = breadth - 1
+        es, ed, et = pltpu.roll(s, back, 1), pltpu.roll(d, back, 1), pltpu.roll(t, back, 1)
+        ref[AS, here, :] = es - s
+        ref[BT, here, :] = et + t
+        ref[AT, here, :] = et - t
+        ref[BD, here, :] = ed + d
 
     def velocity_tile(ref, g, folded=None, ghost=None, last=None):
-        here = slice(PAD + 8 * g, PAD + 8 * g + 8)
+        here = tile(g)
         north = slice(PAD + 8 * g + 1, PAD + 8 * g + 9)
-        s, d, t = ref[S, here, :], ref[D, here, :], ref[T, here, :]
-        ns, nd, nt = ref[S, north, :], ref[D, north, :], ref[T, north, :]
+        kinds = AS, BT, AT, BD
+        above = [ref[f, north, :] for f in kinds]
         if last is not None:
-            ns, nd, nt = (
-                jnp.where(last_line, spread(ref, f, last), n)
-                for f, n in ((S, ns), (D, nd), (T, nt))
-            )
+            above = [jnp.where(last_line, spread(ref, f, last), x) for f, x in zip(kinds, above)]
         if folded is not None:
-            ns, nd, nt = (jnp.where(folded, 0.0, n) for n in (ns, nd, nt))
-        ps, dt, pt, dd = s + ns, nt - t, t + nt, nd - d
-        back = breadth - 1
-        es, et = pltpu.roll(ps, back, 1) - ps, dt + pltpu.roll(dt, back, 1)
-        ft, fd = pltpu.roll(pt, back, 1) - pt, dd + pltpu.roll(dd, back, 1)
-        if folded is not None:
-            es, et, ft, fd = (
-                value + jnp.where(folded, line, 0.0)
-                for value, line in zip((es, et, ft, fd), ghost)
-            )
+            above = [jnp.where(folded, line, x) for line, x in zip(ghost, above)]
+        es, et = above[0] + ref[AS, here, :], above[1] - ref[BT, here, :]
+        ft, fd = above[2] + ref[AT, here, :], above[3] - ref[BD, here, :]
         fw, fh = ref[FW, here, :], ref[FH, here, :]
         x = ref[U, here, :] + (fw * es + fh * et)
         y = ref[V, here, :] + (fw * ft + fh * fd)
@@ -620,31 +642,42 @@
         return found
 
     def cycle(first, stresses, velocities):
+        inner = range(first, tall - first)
+        for g in range(first, stresses):
+            differ_velocity(main, g)
+            if g in inner:
+                differ_velocity(side, g)
+        for g in range(first, stresses):
+            far = near_first + 15
+            stress_tile(main, g, fold_south if g == near else None, far)
+            if g in inner:
+                on = fold_south_side if g == near - skip else None
+                stress_tile(side, g, on, far - shift)
+        ghosts = fold()
+        for g in range(first, velocities):
+            if g in (near - 1, near):
+                velocity_tile(main, g, fold_north, ghosts[g - near + 1])
+            else:
+                velocity_tile(main, g, last=near_first if g == total - 1 else None)
+            b = g + skip
+            if g not in inner:
+                continue
+            if b in (near - 1, near):
+                velocity_tile(side, g, fold_north_side, ghosts[2 + b - near + 1])
+            else:
+                last = near_first - shift if g == tall - 1 else None
+                velocity_tile(side, g, last=last)
+
+    def repeat(times, unroll, *ranges, final=None):
         def body(_, carry):
-            for g in range(first, total):
-                if g < stresses:
-                    on = g == near
-                    far = near_first + 15
-                    stress_tile(main, g, fold_south if on else None, far)
-                    if g < tall - first:
-                        on = g == near - skip
-                        stress_tile(side, g, fold_south_side if on else None, far - shift)
-            ghosts = fold()
-            for g in range(first, velocities):
-                if g in (near - 1, near):
-                    velocity_tile(main, g, fold_north, ghosts[g - near + 1])
-                else:
-                    velocity_tile(main, g, last=near_first if g == total - 1 else None)
-                b = g + skip
-                if g < tall - first:
-                    if b in (near - 1, near):
-                        velocity_tile(side, g, fold_north_side, ghosts[2 + b - near + 1])
-                    else:
-                        last = near_first - shift if g == tall - 1 else None
-                        velocity_tile(side, g, last=last)
+            for n in range(unroll):
+                cycle(*(ranges if n < unroll - 1 or not final else final))
             return carry
 
-        return body
+        if times == unroll:
+            body(0, 0)
+        else:
+            lax.fori_loop(0, times // unroll, body, 0)
 
     def relay(k, part):
         source = lax.rem(r + nr - 2 * (k + 1), nr)
@@ -667,13 +700,12 @@
                     relays[2 * k + part].start()
 
     wide = SUB - 8
-    lax.fori_loop(0, wide, cycle(0, total, total), 0)
+    inside = (1, total - 1, total - 1)
+    repeat(wide, 2, 0, total, total)
     pass_on((0, 1), True)
-    lax.fori_loop(0, 4, cycle(1, total - 1, total - 1), 0)
-    pass_on((0,), False)
-    lax.fori_loop(0, SUB - wide - 5, cycle(1, total - 1, total - 1), 0)
-    pass_on((1,), False)
-    cycle(1, total - 1, near)(0, 0)
+    repeat(4, 2, *inside)
+    pass_on((0, 1), False)
+    repeat(SUB - wide - 4, 4, *inside, final=(1, total - 1, near))
 
     keep = lane < cut
     for k in range(groups):

time: 17.6 us -> 17.1 us (0.972)
  the two profiles are of different devices: /device:TPU:0 before, /device:TPU:1 now
where the time goes in v1:
time: 17.1 us; the launch traced here: 16.9 us
  Pallas kernels  16.3 us (95%)
  between operations  0.64 us (4%)
    pallas_call x1, Pallas kernels, shards(): pl.pallas_call(functools.partial(kernel, nr, nc), out_shape=(jax.ShapeDty...  15 us
    pallas_call x1, Pallas kernels, shards(): pl.pallas_call(place, out_shape=(jax.ShapeDtypeStruct((1,) + strips.shape...  1.31 us

profile of v1, /device:TPU:1, one launch (start us, length us, event | category | flops | bytes accessed | tf_op | source)
XLA Modules:
  0.0 16.9 jit_solution(479399317781353540)
XLA Ops:
  0.6 15.0 %shard_map.130 = (f32[2,64,128]{2,1,0:T(8,128)S(1)}, f32[3,64,128]{2,1,0:T(8,128)S(1)}, f32[10,256,128]{2,1,0:T(8,128)S(1)}, s32[1,8]{1,0:T(1,128)S(1)}) custom-call(f32[2,64,128]{2,1,0:T(8,128)} %vel_in.1, f32[3,64,128]{2,1,0:T(8,128)} %str_in.1, f32[2,64,128]{2,1,0:T(8,128)} %wind_in.1, f32[2,64,128]{2,1,0:T(8,128)} %cur_in.1, f32[5,64,128]{2,1,0:T(8,128)} %area_in.1, ...), custom_call_target="tpu_custom_call" | custom-call | flops 29491200 | bytes 763904 | tf_op jit(solution)/shard_map/pallas_call | solution.py:814
  15.6 1.3 %shard_map.131 = (f32[1,10,256,128]{3,2,1,0:T(8,128)}, f32[2,64,128]{2,1,0:T(8,128)}, f32[3,64,128]{2,1,0:T(8,128)}) custom-call(f32[10,256,128]{2,1,0:T(8,128)S(1)} %get-tuple-element.10.strips, f32[2,64,128]{2,1,0:T(8,128)S(1)} %get-tuple-element.11.vel, f32[3,64,128]{2,1,0:T(8,128)S(1)} %get-tuple-element.12.stress, s32[1,8]{1,0:T(1,128)S(1)} %get-tuple-element.13.writer), custom_call_target="tpu_custom_call" | custom-call | tf_op jit(solution)/shard_map/pallas_call | solution.py:859

commit v2 on v1

--- a/solution.py
+++ b/solution.py
@@ -10,10 +10,9 @@
 SUB = 12
 PAD = 8
 FIELDS = 11
-STORED = 22
+STORED = 23
 U, V, S, D, T, GU, GV, INERTIA, STRENGTH, HW, HH, BETA, FW, FH, *DIFFS = range(STORED)
-ALPHA = INERTIA
-AU, BU, AV, BV, AS, BT, AT, BD = DIFFS
+ALPHA, AU, BU, AV, BV, AS, BT, AT, BD = DIFFS
 TINY = 1.1754944e-38
 
 strength_scale = 4.0
@@ -242,7 +241,6 @@
     lane = lax.broadcasted_iota(jnp.int32, (8, breadth), 1)
     sub = lax.broadcasted_iota(jnp.int32, (8, breadth), 0)
     zero = jnp.zeros((8, breadth), jnp.float32)
-    left_half = lane < half
     for f in range(5):
         for ref, end in ((main, PAD + rows), (side, PAD + 8 * tall)):
             ref[f, 0:PAD, :] = zero
@@ -277,21 +275,24 @@
 
     bottom = slice(0, tiles)
     upper = slice(tiles, 2 * tiles)
-    vals_top = vals.at[:, height - hr : height, :]
-    vals_bottom = vals.at[:, 0:hr, :]
+    vals_top = vals.at[:, height - SUB : height, :]
+    vals_bottom = vals.at[:, 0:SUB, :]
+    near_s = land_s.at[:, hr - SUB : hr, :]
+    near_n = land_n.at[:, 0:SUB, :]
+    near_fold = land_n.at[:, hr - SUB : hr, :]
     to_west = halo(0, pack_w, mid_e, r, west)
     to_east = halo(1, pack_e, mid_w, r, east)
     up = [
-        halo(2, vals_top, land_s, r + 1, c),
+        halo(2, vals_top, near_s, r + 1, c),
         halo(4, pack_w.at[upper], low_e, r + 1, west),
         halo(5, pack_e.at[upper], low_w, r + 1, east),
     ]
     down = [
-        halo(3, vals_bottom, land_n, r - 1, c),
+        halo(3, vals_bottom, near_n, r - 1, c),
         halo(6, pack_w.at[bottom], high_e, r - 1, west),
         halo(7, pack_e.at[bottom], high_w, r - 1, east),
     ]
-    over = remote(vals_top, land_n, send_sem.at[8], recv_sem.at[3], r, mirror)
+    over = remote(vals_top, near_fold, send_sem.at[8], recv_sem.at[3], r, mirror)
     over_w = remote(pack_w.at[upper], high_e, send_sem.at[9], recv_sem.at[6], r, m_w)
     over_e = remote(pack_e.at[upper], high_w, send_sem.at[10], recv_sem.at[7], r, m_e)
 
@@ -395,16 +396,16 @@
         high_w[...] = pack_e[upper]
 
     def send_beside(mid, across, other, folded):
+        @pl.when(above_bottom)
+        def _():
+            down[across].start()
+
         mid.start()
 
         @pl.when(not_top)
         def _():
             up[across].start()
 
-        @pl.when(above_bottom)
-        def _():
-            down[across].start()
-
         @pl.when(other)
         def _():
             folded.start()
@@ -437,9 +438,9 @@
         return [(b, n) for b, n in ((g, 0), (g - skip, 1)) if 0 <= b < tall]
 
     def fill(g, f, value):
-        main[f, tile(g), :] = roll(value, SUB)
+        pltpu.store(main.at[f, tile(g), :], roll(value, SUB), mask=lane >= SUB)
         for b, right in homes(g):
-            mask = lane >= half if right else left_half
+            mask = (lane >= half) & (lane < breadth - SUB) if right else lane < half - SUB
             pltpu.store(side.at[f, tile(b), :], roll(value, right * half - base), mask=mask)
 
     for k in range(groups):
@@ -452,26 +453,24 @@
         low_e[...] = jnp.zeros(low_e.shape, jnp.float32)
         low_w[...] = jnp.zeros(low_w.shape, jnp.float32)
 
-    swap = is_top.astype(jnp.int32)
+    def fill_north(swap):
+        for g in range(deep):
+            line = deep - 1 - g if swap else g
+            for f in range(FIELDS):
+                fill(deep + groups + g, f, land_n[f, 8 * line : 8 * line + 8, :])
 
     @pl.when(above_bottom)
     def _():
         up[0].wait_recv()
 
-    @pl.when(not_top)
-    def _():
-        down[0].wait_recv()
-
-    @pl.when(is_top)
-    def _():
-        over.wait_recv()
-
     for g in range(deep):
-        line = g + swap * (deep - 1 - 2 * g)
-        from_n = pl.ds(pl.multiple_of(8 * line, 8), 8)
         for f in range(FIELDS):
             fill(g, f, land_s[f, 8 * g : 8 * g + 8, :])
-            fill(deep + groups + g, f, land_n[f, from_n, :])
+
+    @pl.when(not_top)
+    def _():
+        down[0].wait_recv()
+        fill_north(False)
 
     def edges(span, source, first, origin):
         for g in span:
@@ -532,6 +531,15 @@
             pltpu.store(main.at[f, tile(g), :], roll(value, SUB - at), mask=lane < SUB)
         for g in span[0]:
             derive(main, tile(g))
+
+    @pl.when(is_top)
+    def _():
+        over.wait_recv()
+        fill_north(True)
+        for g in highs:
+            derive(main, tile(g))
+            for b, _ in homes(g):
+                derive(side, tile(b))
 
     near = deep + groups
     near_first = PAD + 8 * near

time: 17.1 us -> 16.6 us (0.971)
  the two profiles are of different devices: /device:TPU:1 before, /device:TPU:0 now
where the time goes in v2:
time: 16.6 us; the launch traced here: 16.4 us
  Pallas kernels  15.8 us (95%)
  between operations  0.64 us (4%)
    pallas_call x1, Pallas kernels, shards(): pl.pallas_call(functools.partial(kernel, nr, nc), out_shape=(jax.ShapeDty...  14.5 us
    pallas_call x1, Pallas kernels, shards(): pl.pallas_call(place, out_shape=(jax.ShapeDtypeStruct((1,) + strips.shape...  1.31 us

profile of v2, /device:TPU:0, one launch (start us, length us, event | category | flops | bytes accessed | tf_op | source)
XLA Modules:
  0.0 16.4 jit_solution(10609296123675938334)
XLA Ops:
  0.6 14.5 %shard_map.130 = (f32[2,64,128]{2,1,0:T(8,128)S(1)}, f32[3,64,128]{2,1,0:T(8,128)S(1)}, f32[10,256,128]{2,1,0:T(8,128)S(1)}, s32[1,8]{1,0:T(1,128)S(1)}) custom-call(f32[2,64,128]{2,1,0:T(8,128)} %vel_in.1, f32[3,64,128]{2,1,0:T(8,128)} %str_in.1, f32[2,64,128]{2,1,0:T(8,128)} %wind_in.1, f32[2,64,128]{2,1,0:T(8,128)} %cur_in.1, f32[5,64,128]{2,1,0:T(8,128)} %area_in.1, ...), custom_call_target="tpu_custom_call" | custom-call | flops 29491200 | bytes 763904 | tf_op jit(solution)/shard_map/pallas_call | solution.py:822
  15.1 1.3 %shard_map.131 = (f32[1,10,256,128]{3,2,1,0:T(8,128)}, f32[2,64,128]{2,1,0:T(8,128)}, f32[3,64,128]{2,1,0:T(8,128)}) custom-call(f32[10,256,128]{2,1,0:T(8,128)S(1)} %get-tuple-element.10.strips, f32[2,64,128]{2,1,0:T(8,128)S(1)} %get-tuple-element.11.vel, f32[3,64,128]{2,1,0:T(8,128)S(1)} %get-tuple-element.12.stress, s32[1,8]{1,0:T(1,128)S(1)} %get-tuple-element.13.writer), custom_call_target="tpu_custom_call" | custom-call | tf_op jit(solution)/shard_map/pallas_call | solution.py:867

commit v3 on v2

--- a/solution.py
+++ b/solution.py
@@ -520,10 +520,10 @@
     for b in range(tall):
         derive(side, tile(b))
 
-    for n, (source, span) in enumerate(zip((mid_w, low_w, high_w), spans)):
-        if n == 0:
+    for source, span in zip((low_w, high_w, mid_w), spans[1:] + spans[:1]):
+        if source is mid_w:
             to_east.wait_recv()
-        elif n == 1:
+        elif source is low_w:
             await_low(2)
         else:
             await_high(2, other_e, over_e)

time: 16.6 us -> 16.5 us (level)
  no operation moved by 1% of the time
where the time goes in v3:
time: 16.5 us; the launch traced here: 16.4 us
  Pallas kernels  15.7 us (95%)
  between operations  0.64 us (4%)
    pallas_call x1, Pallas kernels, shards(): pl.pallas_call(functools.partial(kernel, nr, nc), out_shape=(jax.ShapeDty...  14.4 us
    pallas_call x1, Pallas kernels, shards(): pl.pallas_call(place, out_shape=(jax.ShapeDtypeStruct((1,) + strips.shape...  1.31 us

profile of v3, /device:TPU:0, one launch (start us, length us, event | category | flops | bytes accessed | tf_op | source)
XLA Modules:
  0.0 16.4 jit_solution(7616059734794968881)
XLA Ops:
  0.6 14.4 %shard_map.130 = (f32[2,64,128]{2,1,0:T(8,128)S(1)}, f32[3,64,128]{2,1,0:T(8,128)S(1)}, f32[10,256,128]{2,1,0:T(8,128)S(1)}, s32[1,8]{1,0:T(1,128)S(1)}) custom-call(f32[2,64,128]{2,1,0:T(8,128)} %vel_in.1, f32[3,64,128]{2,1,0:T(8,128)} %str_in.1, f32[2,64,128]{2,1,0:T(8,128)} %wind_in.1, f32[2,64,128]{2,1,0:T(8,128)} %cur_in.1, f32[5,64,128]{2,1,0:T(8,128)} %area_in.1, ...), custom_call_target="tpu_custom_call" | custom-call | flops 29491200 | bytes 763904 | tf_op jit(solution)/shard_map/pallas_call | solution.py:822
  15.1 1.3 %shard_map.131 = (f32[1,10,256,128]{3,2,1,0:T(8,128)}, f32[2,64,128]{2,1,0:T(8,128)}, f32[3,64,128]{2,1,0:T(8,128)}) custom-call(f32[10,256,128]{2,1,0:T(8,128)S(1)} %get-tuple-element.10.strips, f32[2,64,128]{2,1,0:T(8,128)S(1)} %get-tuple-element.11.vel, f32[3,64,128]{2,1,0:T(8,128)S(1)} %get-tuple-element.12.stress, s32[1,8]{1,0:T(1,128)S(1)} %get-tuple-element.13.writer), custom_call_target="tpu_custom_call" | custom-call | tf_op jit(solution)/shard_map/pallas_call | solution.py:867
